TPU v7x, 32 devices: a whole 2x2x4 slice. The times are simulated.
32 devices in a mesh: dp: 16 (over z, y, x), mp: 2 (over core).
Axes of the slice: x: 2, y: 2, z: 4, core: 2. Of those that a mesh axis runs over, the one named last changes fastest.
Arguments:
- inputs: bfloat16 [2048, 1792], P('dp', 'mp'), may hold values from -6 to 6
- cotangent: bfloat16 [2048, 1792], P('dp', 'mp'), may hold values from -6 to 6
- gate_weight: bfloat16 [9472, 1792], P(('mp', 'dp')), may hold values from -0.125 to 0.125
- up_weight: bfloat16 [9472, 1792], P(('mp', 'dp')), may hold values from -0.125 to 0.125
- down_weight: bfloat16 [9472, 1792], P(('mp', 'dp')), may hold values from -0.0625 to 0.0625
Outputs:
- input_grad: bfloat16 [2048, 1792], P('dp', 'mp')
- gate_grad: bfloat16 [9472, 1792], P(('mp', 'dp'))
All inputs are finite; a program needn't handle non-finite values.
Results may differ from a plain program's by a relative error of at most 0.009.
Values may be sent and summed in bfloat16 or wider, within the bound.
A program may use at most 320 MiB of HBM per device.

v0:
```python
import jax
import jax.numpy as jnp
from jax import lax
from jax.sharding import PartitionSpec as P


def tdot(left, right):
    return lax.dot_general(
        left, right, (((0,), (0,)), ((), ())), preferred_element_type=jnp.float32
    )


def rdot(left, right):
    return lax.dot_general(
        left, right, (((1,), (1,)), ((), ())), preferred_element_type=jnp.float32
    )


def per_device(inputs, cotangent, gate_weight, up_weight, down_weight):

    def tokens(block):
        rows = lax.all_gather(block, "dp", axis=0, tiled=True)
        return lax.all_gather(rows, "mp", axis=1, tiled=True)

    full_in = tokens(inputs)
    full_cot = tokens(cotangent)
    gate = rdot(full_in, gate_weight)
    up = rdot(full_in, up_weight)
    dhidden = rdot(full_cot, down_weight)
    sig = jax.nn.sigmoid(gate)
    act = gate * sig
    dup = (dhidden * act).astype(jnp.bfloat16)
    dgate = (dhidden * up * sig * (1.0 + gate * (1.0 - sig))).astype(jnp.bfloat16)
    partial = jnp.dot(dgate, gate_weight, preferred_element_type=jnp.float32)
    partial = partial + jnp.dot(dup, up_weight, preferred_element_type=jnp.float32)
    partial = lax.psum_scatter(partial.astype(jnp.bfloat16), "mp", scatter_dimension=1, tiled=True)
    input_grad = lax.psum_scatter(partial, "dp", scatter_dimension=0, tiled=True)
    gate_grad = tdot(dgate, full_in).astype(jnp.bfloat16)
    return (input_grad, gate_grad)


def solution(mesh):
    placed = (
        P("dp", "mp"),
        P("dp", "mp"),
        P(("mp", "dp"), None),
        P(("mp", "dp"), None),
        P(("mp", "dp"), None),
    )
    return jax.shard_map(
        per_device,
        mesh=mesh,
        in_specs=placed,
        out_specs=(P("dp", "mp"), P(("mp", "dp"), None)),
        check_vma=False,
    )
```

profile of v0, /device:TPU:0, one launch (start us, length us, event | category | flops | bytes accessed | tf_op | source)
XLA Modules:
  0.0 350.5 jit_solution(10456565937666532263)
XLA Ops:
  7.2 0.0 copy-start
  7.2 0.0 all-gather.5.cloned.1.call-start
  7.2 0.7 all-gather.5.cloned.1.call-update
  7.9 0.0 all-gather.9.cloned.1.call-start
  8.0 0.7 all-gather.9.cloned.1.call-update
  8.7 0.0 all-gather.7.cloned.1.call-start
  8.7 76.4 %all-gather.5.cloned.1.call-done = bf16[2048,896]{1,0:T(8,128)(2,1)} async-done(((bf16[128,896]{1,0:T(8,128)(2,1)}), bf16[2048,896]{1,0:T(8,128)(2,1)}) %all-gather.5.cloned.1.call-update) | async-done | bytes 3670032 | tf_op jit(solution)/shard_map/all_gather | solution.py:22
  85.1 0.0 all-gather.7.cloned.1.call-update
  85.1 0.0 all-gather.11.cloned.1.call-start
  85.2 72.9 %all-gather.9.cloned.1.call-done = bf16[2048,896]{1,0:T(8,128)(2,1)} async-done(((bf16[128,896]{1,0:T(8,128)(2,1)}), bf16[2048,896]{1,0:T(8,128)(2,1)}) %all-gather.9.cloned.1.call-update) | async-done | bytes 3670032 | tf_op jit(solution)/shard_map/all_gather | solution.py:22
  158.1 0.0 all-gather.11.cloned.1.call-update
  158.1 0.0 reduce-scatter.7.cloned.1.call-start
  158.1 18.3 %all-gather.7.cloned.1.call-done = bf16[2048,1792]{1,0:T(8,128)(2,1)} async-done(((bf16[2048,896]{1,0:T(8,128)(2,1)}), bf16[2048,1792]{1,0:T(8,128)(2,1)}) %all-gather.7.cloned.1.call-update) | async-done | bytes 7340048 | tf_op jit(solution)/shard_map/all_gather | solution.py:23
  176.4 5.7 %fusion.5 = f32[2048,296]{0,1:T(8,128)S(1)} fusion(bf16[2048,1792]{1,0:T(8,128)(2,1)} %all-gather.7.cloned.1.call-done, bf16[296,1792]{1,0:T(8,128)(2,1)} %param.9), kind=kOutput, calls=%fused_computation.10 | convolution fusion | flops 2172649472 | bytes 10825728 | tf_op jit(solution)/shard_map/dot_general | solution.py:14
  182.1 15.1 %all-gather.11.cloned.1.call-done = bf16[2048,1792]{1,0:T(8,128)(2,1)} async-done(((bf16[2048,896]{1,0:T(8,128)(2,1)}), bf16[2048,1792]{1,0:T(8,128)(2,1)}) %all-gather.11.cloned.1.call-update) | async-done | bytes 7340048 | tf_op jit(solution)/shard_map/all_gather | solution.py:23
  197.2 0.0 copy-done
  197.2 0.0 copy-start.4
  197.2 0.0 copy-start.5
  197.2 5.6 %fusion.6 = f32[2048,296]{0,1:T(8,128)S(1)} fusion(bf16[2048,1792]{1,0:T(8,128)(2,1)} %all-gather.11.cloned.1.call-done, bf16[296,1792]{1,0:T(8,128)(2,1)S(1)} %copy-done), kind=kOutput, calls=%fused_computation.11 | convolution fusion | flops 2172649472 | bytes 10825728 | tf_op jit(solution)/shard_map/dot_general | solution.py:14
  202.9 0.0 copy-done.4
  202.9 0.0 copy-done.5
  202.9 2.8 fusion.2
  205.7 0.0 copy-start.2
  205.7 7.4 %fusion.7 = f32[2048,1792]{1,0:T(8,128)} fusion(bf16[2048,296]{0,1:T(8,128)(2,1)S(1)} %fusion.2, bf16[296,1792]{1,0:T(8,128)(2,1)S(1)} %copy-done), kind=kOutput, calls=%fused_computation.12 | convolution fusion | flops 2172649472 | bytes 16953344 | tf_op jit(solution)/shard_map/dot_general | solution.py:34
  213.1 0.0 copy-done.2
  213.1 9.3 %add_convert_fusion = bf16[2048,1792]{1,0:T(8,128)(2,1)} fusion(f32[2048,1792]{1,0:T(8,128)} %fusion.7, bf16[296,1792]{1,0:T(8,128)(2,1)S(1)} %copy-done.4, f32[2048,296]{0,1:T(8,128)S(1)} %fusion.5, f32[2048,296]{0,1:T(8,128)S(1)} %fusion.6), kind=kOutput, calls=%fused_computation | convolution fusion | flops 2183626752 | bytes 27930624 | tf_op jit(solution)/shard_map/dot_general | solution.py:35
  222.4 10.5 %copy.7 = bf16[2048,1792]{0,1:T(8,128)(2,1)} copy(bf16[2048,1792]{1,0:T(8,128)(2,1)} %add_convert_fusion) | data formatting | bytes 14680064
  232.9 0.0 reduce-scatter.7.cloned.1.call-update
  232.9 0.0 reduce-scatter.5.cloned.1.call-start
  233.0 17.4 %reduce-scatter.7.cloned.1.call-done = bf16[896,2048]{1,0:T(8,128)(2,1)} async-done(((bf16[1792,2048]{1,0:T(8,128)(2,1)}), bf16[896,2048]{1,0:T(8,128)(2,1)}) %reduce-scatter.7.cloned.1.call-update) | async-done | bytes 3670032
  250.4 6.1 %copy.8 = bf16[2048,896]{1,0:T(8,128)(2,1)} copy(bf16[2048,896]{0,1:T(8,128)(2,1)} %bitcast.14) | data formatting | bytes 7340032
  256.5 0.0 copy-start.3
  256.5 0.0 reduce-scatter.5.cloned.1.call-update
  256.5 1.3 copy-done.3
  257.8 0.0 copy-start.1
  257.8 6.5 %convolution_convert_fusion = bf16[296,1792]{1,0:T(8,128)(2,1)} fusion(bf16[2048,296]{0,1:T(8,128)(2,1)S(1)} %copy-done.3, bf16[2048,1792]{1,0:T(8,128)(2,1)} %all-gather.11.cloned.1.call-done), kind=kOutput, calls=%fused_computation.5 | convolution fusion | flops 2173179904 | bytes 9613312 | tf_op jit(solution)/shard_map/dot_general | solution.py:8
  264.3 79.3 %reduce-scatter.5.cloned.1.call-done = bf16[128,896]{1,0:T(8,128)(2,1)} async-done(((bf16[2048,896]{1,0:T(8,128)(2,1)}), bf16[128,896]{1,0:T(8,128)(2,1)}) %reduce-scatter.5.cloned.1.call-update) | async-done | bytes 229392 | tf_op jit(solution)/shard_map/reduce_scatter | solution.py:37
  343.6 0.0 copy-done.1
Async XLA Ops:
  7.2 190.1 %copy-start = (bf16[296,1792]{1,0:T(8,128)(2,1)S(1)}, bf16[296,1792]{1,0:T(8,128)(2,1)}, u32[]{:S(2)}) copy-start(bf16[296,1792]{1,0:T(8,128)(2,1)} %param.7) | copy-start | bytes 3182596
  7.2 77.9 %all-gather.5.cloned.1.call-start = ((), (), s32[]{:S(2)}) async-start(), calls=%async_computation.2 | async-start | bytes 3899392 | tf_op jit(solution)/shard_map/all_gather | solution.py:22
  7.9 150.2 %all-gather.9.cloned.1.call-start = ((), (), s32[]{:S(2)}) async-start(), calls=%async_computation.4 | async-start | bytes 3899392 | tf_op jit(solution)/shard_map/all_gather | solution.py:22
  8.7 167.7 %all-gather.7.cloned.1.call-start = ((), (), s32[]{:S(2)}) async-start(), calls=%async_computation.3 | async-start | bytes 11010048 | tf_op jit(solution)/shard_map/all_gather | solution.py:23
  85.1 112.1 %all-gather.11.cloned.1.call-start = ((), (), s32[]{:S(2)}) async-start(), calls=%async_computation.5 | async-start | bytes 11010048 | tf_op jit(solution)/shard_map/all_gather | solution.py:23
  158.1 92.3 %reduce-scatter.7.cloned.1.call-start = ((), (), s32[]{:S(2)}) async-start(), calls=%async_computation.7 | async-start | bytes 11010048
  197.2 5.6 %copy-start.4 = (bf16[296,1792]{1,0:T(8,128)(2,1)S(1)}, bf16[296,1792]{1,0:T(8,128)(2,1)}, u32[]{:S(2)}) copy-start(bf16[296,1792]{1,0:T(8,128)(2,1)} %param.8) | copy-start | bytes 3182596
  197.2 5.6 %copy-start.5 = (bf16[2048,1792]{1,0:T(8,128)(2,1)S(1)}, bf16[2048,1792]{1,0:T(8,128)(2,1)}, u32[]{:S(2)}) copy-start(bf16[2048,1792]{1,0:T(8,128)(2,1)} %all-gather.11.cloned.1.call-done) | copy-start | bytes 22020100
  205.7 7.4 %copy-start.2 = (bf16[2048,296]{0,1:T(8,128)(2,1)}, bf16[2048,296]{0,1:T(8,128)(2,1)S(1)}, u32[]{:S(2)}) copy-start(bf16[2048,296]{0,1:T(8,128)(2,1)S(1)} %fusion.2) | copy-start | bytes 3637252
  232.9 110.7 %reduce-scatter.5.cloned.1.call-start = ((), (), s32[]{:S(2)}) async-start(), calls=%async_computation.6 | async-start | bytes 3899392 | tf_op jit(solution)/shard_map/reduce_scatter | solution.py:37
  256.5 1.3 copy-start.3
  257.8 85.9 %copy-start.1 = (bf16[296,1792]{1,0:T(8,128)(2,1)S(1)}, bf16[296,1792]{1,0:T(8,128)(2,1)}, u32[]{:S(2)}) copy-start(bf16[296,1792]{1,0:T(8,128)(2,1)} %param.7) | copy-start | bytes 3182596
Sparse Core Ops, SparseCore 0:
  10.7 74.3 all-gather.4
  87.9 70.1 all-gather.8
  159.6 16.7 all-gather.6
  177.8 19.3 all-gather.10
  233.0 17.3 reduce-scatter.6
  256.6 86.9 reduce-scatter.4
where the time goes:
time: 351 us; the launch traced here: 350 us
  waiting for transfers between devices  281 us (80%)
  matrix products  37.3 us (11%)
  local copies, waits for them, and re-layouts  17.9 us (5%)
  between operations  14.2 us (4%)
    all_gather x2, waiting for transfers between devices, tokens(): rows = lax.all_gather(block, 'dp', axis=0, tiled=True)  149 us
    reduce_scatter x1, waiting for transfers between devices, per_device(): lax.psum_scatter(partial, 'dp', scatter_dimension=0, tiled=True)  79.3 us
    all_gather x2, waiting for transfers between devices, tokens(): return lax.all_gather(rows, 'mp', axis=1, tiled=True)  33.4 us
    unnamed x7, waiting for transfers between devices  18.9 us
    unnamed x14, local copies, waits for them, and re-layouts  17.9 us
    dot_general x3, matrix products, rdot(): lax.dot_general(left, right, (((1,), (1,)), ((), ())), preferred_element_...  14.2 us
    dot_general x1, matrix products, per_device(): jnp.dot(dup, up_weight, preferred_element_type=jnp.float32)  9.27 us
    dot_general x1, matrix products, per_device(): partial = jnp.dot(dgate, gate_weight, preferred_element_type=jnp.float32)  7.38 us
  transfers between devices with their start and end apart: 6, of which 6 were waited for; matrix products, arithmetic and copies ran while one was open for 3% of the time, Pallas kernels for 0%

commit v1 on v0

--- a/solution.py
+++ b/solution.py
@@ -2,6 +2,11 @@
 import jax.numpy as jnp
 from jax import lax
 from jax.sharding import PartitionSpec as P
+
+
+def gathered_along(x, name, dim):
+    pieces = lax.all_gather(x, name)
+    return jnp.concatenate(pieces, axis=dim)
 
 
 def tdot(left, right):
@@ -20,7 +25,7 @@
 
     def tokens(block):
         rows = lax.all_gather(block, "dp", axis=0, tiled=True)
-        return lax.all_gather(rows, "mp", axis=1, tiled=True)
+        return gathered_along(rows, "mp", 1)
 
     full_in = tokens(inputs)
     full_cot = tokens(cotangent)

time: 351 us -> 366 us (1.043)
  local copies, waits for them, and re-layouts: 17.9 us -> 39.3 us
  waiting for transfers between devices: 281 us -> 277 us
    reshape x0 -> x2, local copies, waits for them, and re-layouts: none -> 22.7 us  [gathered_along(): return jnp.concatenate(pieces, axis=dim)]
    all_gather x2, waiting for transfers between devices: 33.4 us -> 27.9 us  [gathered_along(): pieces = lax.all_gather(x, name)]
    unnamed x14 -> x12, local copies, waits for them, and re-layouts: 17.9 us -> 16.6 us
  transfers between devices with their start and end apart: 6 -> 6, of which waited for: 6 -> 6; matrix products, arithmetic and copies ran while one was open for 3% -> 5% of each run, Pallas kernels for 0% -> 0%
where the time goes in v1:
time: 366 us; the launch traced here: 365 us
  waiting for transfers between devices  277 us (76%)
  local copies, waits for them, and re-layouts  39.3 us (11%)
  matrix products  34.6 us (9%)
  between operations  14.2 us (4%)
    all_gather x2, waiting for transfers between devices, tokens(): rows = lax.all_gather(block, 'dp', axis=0, tiled=True)  149 us
    reduce_scatter x1, waiting for transfers between devices, per_device(): lax.psum_scatter(partial, 'dp', scatter_dimension=0, tiled=True)  80.5 us
    all_gather x2, waiting for transfers between devices, gathered_along(): pieces = lax.all_gather(x, name)  27.9 us
    reshape x2, local copies, waits for them, and re-layouts, gathered_along(): return jnp.concatenate(pieces, axis=dim)  22.7 us
    unnamed x7, waiting for transfers between devices  18.8 us
    unnamed x12, local copies, waits for them, and re-layouts  16.6 us
    dot_general x3, matrix products, rdot(): lax.dot_general(left, right, (((1,), (1,)), ((), ())), preferred_element_...  11.3 us
    dot_general x1, matrix products, per_device(): jnp.dot(dup, up_weight, preferred_element_type=jnp.float32)  9.28 us
  transfers between devices with their start and end apart: 6, of which 6 were waited for; matrix products, arithmetic and copies ran while one was open for 5% of the time, Pallas kernels for 0%

profile of v1, /device:TPU:0, one launch (start us, length us, event | category | flops | bytes accessed | tf_op | source)
XLA Modules:
  0.0 364.9 jit_solution(13433581957209039403)
XLA Ops:
  7.2 0.0 copy-start
  7.2 0.0 all-gather.9.cloned.1.call-start
  7.2 0.7 all-gather.9.cloned.1.call-update
  7.9 0.0 all-gather.7.cloned.1.call-start
  8.0 0.7 all-gather.7.cloned.1.call-update
  8.7 0.0 all-gather.13.cloned.1.call-start
  8.7 76.4 %all-gather.9.cloned.1.call-done = bf16[2048,896]{1,0:T(8,128)(2,1)} async-done(((bf16[128,896]{1,0:T(8,128)(2,1)}), bf16[2048,896]{1,0:T(8,128)(2,1)}) %all-gather.9.cloned.1.call-update) | async-done | bytes 3670032 | tf_op jit(solution)/shard_map/all_gather | solution.py:27
  85.1 0.0 all-gather.13.cloned.1.call-update
  85.1 0.0 all-gather.11.cloned.1.call-start
  85.2 72.9 %all-gather.7.cloned.1.call-done = bf16[2048,896]{1,0:T(8,128)(2,1)} async-done(((bf16[128,896]{1,0:T(8,128)(2,1)}), bf16[2048,896]{1,0:T(8,128)(2,1)}) %all-gather.7.cloned.1.call-update) | async-done | bytes 3670032 | tf_op jit(solution)/shard_map/all_gather | solution.py:27
  158.1 0.0 all-gather.11.cloned.1.call-update
  158.1 0.0 reduce-scatter.7.cloned.1.call-start
  158.1 18.3 %all-gather.13.cloned.1.call-done = bf16[4096,896]{1,0:T(8,128)(2,1)} async-done(((bf16[2048,896]{1,0:T(8,128)(2,1)}), bf16[4096,896]{1,0:T(8,128)(2,1)}) %all-gather.13.cloned.1.call-update) | async-done | bytes 7340048 | tf_op jit(solution)/shard_map/all_gather | solution.py:8
  176.5 11.3 %copy.10 = bf16[2048,2,896]{0,2,1:T(8,128)(2,1)} copy(bf16[2048,2,896]{2,0,1:T(8,128)(2,1)} %bitcast.25) | data formatting | bytes 14680064 | tf_op jit(solution)/shard_map/reshape | solution.py:9
  187.8 9.6 %all-gather.11.cloned.1.call-done = bf16[4096,896]{1,0:T(8,128)(2,1)} async-done(((bf16[2048,896]{1,0:T(8,128)(2,1)}), bf16[4096,896]{1,0:T(8,128)(2,1)}) %all-gather.11.cloned.1.call-update) | async-done | bytes 7340048 | tf_op jit(solution)/shard_map/all_gather | solution.py:8
  197.4 0.0 copy-start.4
  197.4 11.4 %copy.9 = bf16[2048,2,896]{0,2,1:T(8,128)(2,1)} copy(bf16[2048,2,896]{2,0,1:T(8,128)(2,1)} %bitcast.26) | data formatting | bytes 14680064 | tf_op jit(solution)/shard_map/reshape | solution.py:9
  208.8 0.0 copy-done.4
  208.8 0.0 copy-start.2
  208.8 5.7 %fusion.5 = f32[2048,296]{0,1:T(8,128)S(1)} fusion(bf16[2048,1792]{0,1:T(8,128)(2,1)} %bitcast.27, bf16[296,1792]{1,0:T(8,128)(2,1)S(1)} %copy-done.4), kind=kOutput, calls=%fused_computation.10 | convolution fusion | flops 2172649472 | bytes 10825728 | tf_op jit(solution)/shard_map/dot_general | solution.py:19
  214.4 0.0 copy-done
  214.4 0.0 copy-done.2
  214.5 0.0 copy-start.3
  214.5 2.4 fusion.6
  216.9 0.0 copy-done.3
  216.9 3.2 fusion.2
  220.1 7.4 %fusion.7 = f32[2048,1792]{1,0:T(8,128)} fusion(bf16[2048,296]{0,1:T(8,128)(2,1)S(1)} %fusion.2, bf16[296,1792]{1,0:T(8,128)(2,1)S(1)} %copy-done), kind=kOutput, calls=%fused_computation.12 | convolution fusion | flops 2172649472 | bytes 16953344 | tf_op jit(solution)/shard_map/dot_general | solution.py:39
  227.5 9.3 %add_convert_fusion = bf16[2048,1792]{1,0:T(8,128)(2,1)} fusion(f32[2048,1792]{1,0:T(8,128)} %fusion.7, bf16[296,1792]{1,0:T(8,128)(2,1)S(1)} %copy-done.3, f32[2048,296]{0,1:T(8,128)S(1)} %fusion.5, f32[2048,296]{0,1:T(8,128)S(1)} %fusion.6), kind=kOutput, calls=%fused_computation | convolution fusion | flops 2183626752 | bytes 27930624 | tf_op jit(solution)/shard_map/dot_general | solution.py:40
  236.8 10.5 %copy.11 = bf16[2048,1792]{0,1:T(8,128)(2,1)} copy(bf16[2048,1792]{1,0:T(8,128)(2,1)} %add_convert_fusion) | data formatting | bytes 14680064
  247.3 0.0 reduce-scatter.7.cloned.1.call-update
  247.3 0.0 reduce-scatter.5.cloned.1.call-start
  247.4 17.4 %reduce-scatter.7.cloned.1.call-done = bf16[896,2048]{1,0:T(8,128)(2,1)} async-done(((bf16[1792,2048]{1,0:T(8,128)(2,1)}), bf16[896,2048]{1,0:T(8,128)(2,1)}) %reduce-scatter.7.cloned.1.call-update) | async-done | bytes 3670032
  264.7 6.1 %copy.12 = bf16[2048,896]{1,0:T(8,128)(2,1)} copy(bf16[2048,896]{0,1:T(8,128)(2,1)} %bitcast.28) | data formatting | bytes 7340032
  270.8 0.0 reduce-scatter.5.cloned.1.call-update
  270.9 0.0 copy-start.1
  270.9 6.6 %convolution_convert_fusion = bf16[296,1792]{1,0:T(8,128)(2,1)} fusion(bf16[2048,296]{0,1:T(8,128)(2,1)S(1)} %fusion.2, bf16[2048,1792]{0,1:T(8,128)(2,1)} %bitcast.22), kind=kOutput, calls=%fused_computation.5 | convolution fusion | flops 2173179904 | bytes 9613312 | tf_op jit(solution)/shard_map/dot_general | solution.py:13
  277.5 80.5 %reduce-scatter.5.cloned.1.call-done = bf16[128,896]{1,0:T(8,128)(2,1)} async-done(((bf16[2048,896]{1,0:T(8,128)(2,1)}), bf16[128,896]{1,0:T(8,128)(2,1)}) %reduce-scatter.5.cloned.1.call-update) | async-done | bytes 229392 | tf_op jit(solution)/shard_map/reduce_scatter | solution.py:42
  358.0 0.0 copy-done.1
Async XLA Ops:
  7.2 207.3 %copy-start = (bf16[296,1792]{1,0:T(8,128)(2,1)S(1)}, bf16[296,1792]{1,0:T(8,128)(2,1)}, u32[]{:S(2)}) copy-start(bf16[296,1792]{1,0:T(8,128)(2,1)} %param.7) | copy-start | bytes 3182596
  7.2 77.9 %all-gather.9.cloned.1.call-start = ((), (), s32[]{:S(2)}) async-start(), calls=%async_computation.3 | async-start | bytes 3899392 | tf_op jit(solution)/shard_map/all_gather | solution.py:27
  7.9 150.2 %all-gather.7.cloned.1.call-start = ((), (), s32[]{:S(2)}) async-start(), calls=%async_computation.2 | async-start | bytes 3899392 | tf_op jit(solution)/shard_map/all_gather | solution.py:27
  8.7 167.8 %all-gather.13.cloned.1.call-start = ((), (), s32[]{:S(2)}) async-start(), calls=%async_computation.6 | async-start | bytes 11010048 | tf_op jit(solution)/shard_map/all_gather | solution.py:8
  85.1 112.2 %all-gather.11.cloned.1.call-start = ((), (), s32[]{:S(2)}) async-start(), calls=%async_computation.5 | async-start | bytes 11010048 | tf_op jit(solution)/shard_map/all_gather | solution.py:8
  158.1 106.7 %reduce-scatter.7.cloned.1.call-start = ((), (), s32[]{:S(2)}) async-start(), calls=%async_computation.7 | async-start | bytes 11010048
  197.4 11.4 %copy-start.4 = (bf16[296,1792]{1,0:T(8,128)(2,1)S(1)}, bf16[296,1792]{1,0:T(8,128)(2,1)}, u32[]{:S(2)}) copy-start(bf16[296,1792]{1,0:T(8,128)(2,1)} %param.9) | copy-start | bytes 3182596
  208.8 5.7 %copy-start.2 = (bf16[2048,2,896]{0,2,1:T(8,128)(2,1)S(1)}, bf16[2048,2,896]{0,2,1:T(8,128)(2,1)}, u32[]{:S(2)}) copy-start(bf16[2048,2,896]{0,2,1:T(8,128)(2,1)} %copy.10) | copy-start | bytes 22020100
  214.5 2.5 copy-start.3
  247.3 110.7 %reduce-scatter.5.cloned.1.call-start = ((), (), s32[]{:S(2)}) async-start(), calls=%async_computation.4 | async-start | bytes 3899392 | tf_op jit(solution)/shard_map/reduce_scatter | solution.py:42
  270.9 87.2 %copy-start.1 = (bf16[296,1792]{1,0:T(8,128)(2,1)S(1)}, bf16[296,1792]{1,0:T(8,128)(2,1)}, u32[]{:S(2)}) copy-start(bf16[296,1792]{1,0:T(8,128)(2,1)} %param.7) | copy-start | bytes 3182596
Sparse Core Ops, SparseCore 0:
  10.7 74.3 all-gather.8
  87.9 70.1 all-gather.6
  159.6 16.8 all-gather.12
  177.9 19.4 all-gather.10
  247.4 17.2 reduce-scatter.6
  271.0 86.9 reduce-scatter.4
